TPU v7x, 32 devices: a whole 2x2x4 slice. The times are simulated.
32 devices in a mesh: dp: 4 (over y, x), expert: 8 (over z, core).
Axes of the slice: x: 2, y: 2, z: 4, core: 2. Of those that a mesh axis runs over, the one named last changes fastest.
Arguments:
- out_grad: bfloat16 [384, 3072], P(('dp', 'expert')), may hold values from -6 to 6
- layer_input: bfloat16 [384, 3072], P(('dp', 'expert')), may hold values from -6 to 6
- expert_ids: int32 [384, 2], P(('dp', 'expert')), may hold values from 0 to 7, as said below
- gate_prob: float32 [384, 2], P(('dp', 'expert')), may hold values from 0.05 to 1
- w_stack: bfloat16 [3, 3072, 8192], P(None, 'dp', 'expert'), may hold values from -0.109375 to 0.109375
- scale_exps: int32 [3, 24, 64], P(None, 'dp', 'expert'), may hold values from -1 to 1
Outputs:
- input_grad: bfloat16 [384, 3072], P(('dp', 'expert'))
- weight_grads: float32 [3, 3072, 8192], P(None, 'dp', 'expert')
Inputs may be any that keep to these rules, and one draw needn't show every extreme that they name: `expert_ids`: each row names two different experts. In each aligned block of 12 rows (the tokens of one device) between 1 and 3 rows name expert 0, and some blocks have exactly 3 in every draw.
All inputs are finite; a program needn't handle non-finite values.
Results may differ from a plain program's by a relative error of at most 0.015.
Values may be sent and summed in bfloat16 or wider, within the bound.
A program may use at most 128 MiB of HBM per device.

v0:
```python
import jax
import jax.numpy as jnp
from jax import lax
from jax.sharding import PartitionSpec as P

TILE = 128
CAP = 3


def back_project(grad_rows, matrix):
    return lax.dot_general(
        grad_rows, matrix, (((1,), (1,)), ((), ())), preferred_element_type=jnp.float32
    )


def per_device(out_grad, layer_input, expert_ids, gate_prob, w_stack, scale_exps):
    tok_count = out_grad.shape[0]
    routed = expert_ids == 0
    routed_mask = jnp.any(routed, axis=1)
    expert_prob = jnp.sum(jnp.where(routed, gate_prob, 0.0), axis=1)
    slot_index = jnp.cumsum(routed_mask.astype(jnp.int32)) - 1
    places = jnp.arange(CAP, dtype=jnp.int32)
    slot_hit = (slot_index[None, :] == places[:, None]) & routed_mask[None, :]
    source = jnp.sum(
        jnp.where(slot_hit, jnp.arange(tok_count, dtype=jnp.int32)[None, :], 0), axis=1
    )
    slot_valid = jnp.any(slot_hit, axis=1)
    sent_input = jnp.where(slot_valid[:, None], layer_input[source], jnp.zeros((), jnp.bfloat16))
    sent_grad = jnp.where(
        slot_valid[:, None],
        expert_prob[source][:, None] * out_grad[source].astype(jnp.float32),
        0.0,
    ).astype(jnp.bfloat16)
    routed_input, routed_grad = (
        lax.all_gather(sent_input, "expert", axis=0, tiled=True),
        lax.all_gather(sent_grad, "expert", axis=0, tiled=True),
    )
    local_shape = w_stack.shape
    factor = jnp.exp2(scale_exps.astype(jnp.float32))
    scaled = (
        w_stack.astype(jnp.float32).reshape(
            3, local_shape[1] // TILE, TILE, local_shape[2] // TILE, TILE
        )
        * factor[:, :, None, :, None]
    )
    weights = lax.all_gather(
        scaled.reshape(local_shape).astype(jnp.bfloat16), "dp", axis=1, tiled=True
    )
    gate_value = jnp.dot(routed_input, weights[0], preferred_element_type=jnp.float32)
    up_value = jnp.dot(routed_input, weights[1], preferred_element_type=jnp.float32)
    down_back = jnp.dot(routed_grad, weights[2], preferred_element_type=jnp.float32)
    gate_sigmoid = jax.nn.sigmoid(gate_value)
    gate_act = gate_value * gate_sigmoid
    gate_grad = (
        down_back * up_value * gate_sigmoid * (1.0 + gate_value * (1.0 - gate_sigmoid))
    ).astype(jnp.bfloat16)
    up_grad = (down_back * gate_act).astype(jnp.bfloat16)
    hidden = (gate_act * up_value).astype(jnp.bfloat16)
    returned = lax.psum_scatter(
        back_project(gate_grad, weights[0]) + back_project(up_grad, weights[1]),
        "expert",
        scatter_dimension=0,
        tiled=True,
    )
    picked = returned[jnp.clip(slot_index, 0, CAP - 1)]
    input_grad = jnp.where(routed_mask[:, None], picked, 0.0).astype(jnp.bfloat16)
    dp_count = lax.axis_size("dp")
    slot_rows = routed_input.shape[0]
    column_input, column_grad = (
        lax.all_to_all(routed_input, "dp", split_axis=1, concat_axis=0, tiled=True),
        lax.all_to_all(routed_grad, "dp", split_axis=1, concat_axis=0, tiled=True),
    )
    gate_all, up_all, hidden_all = (
        lax.all_gather(gate_grad, "dp", axis=0, tiled=True),
        lax.all_gather(up_grad, "dp", axis=0, tiled=True),
        lax.all_gather(hidden, "dp", axis=0, tiled=True),
    )
    column_input = column_input.reshape(dp_count, slot_rows, -1)
    column_grad = column_grad.reshape(dp_count, slot_rows, -1)
    gate_all = gate_all.reshape(dp_count, slot_rows, -1)
    up_all = up_all.reshape(dp_count, slot_rows, -1)
    hidden_all = hidden_all.reshape(dp_count, slot_rows, -1)
    each_group = jnp.stack(
        [
            jnp.einsum("rkd,rkh->rdh", column_input, gate_all, preferred_element_type=jnp.float32),
            jnp.einsum("rkd,rkh->rdh", column_input, up_all, preferred_element_type=jnp.float32),
            jnp.einsum("rkd,rkh->rdh", column_grad, hidden_all, preferred_element_type=jnp.float32),
        ],
        axis=1,
    )
    rounded = lax.optimization_barrier(each_group.astype(jnp.bfloat16))
    weight_grads = jnp.sum(rounded.astype(jnp.float32), axis=0)
    return (input_grad, weight_grads)


def solution(mesh):
    in_specs = (
        P(("dp", "expert"), None),
        P(("dp", "expert"), None),
        P(("dp", "expert"), None),
        P(("dp", "expert"), None),
        P(None, "dp", "expert"),
        P(None, "dp", "expert"),
    )
    out_specs = (P(("dp", "expert"), None), P(None, "dp", "expert"))
    return jax.shard_map(
        per_device, mesh=mesh, in_specs=in_specs, out_specs=out_specs, check_vma=False
    )
```

profile of v0, /device:TPU:0, one launch (start us, length us, event | category | flops | bytes accessed | tf_op | source)
XLA Modules:
  0.0 335.4 jit_solution(13567222837073245276)
XLA Ops:
  7.9 4.4 %mul.42 = f32[3,6,128,8,128]{4,3,2,1,0:T(8,128)} broadcast(f32[3,6,8]{2,1,0:T(8,128)S(1)} %multiply_exponential_fusion), dimensions={0,1,3} | broadcast | bytes 9437760 | tf_op jit(solution)/shard_map/mul | solution.py:41
  12.4 11.2 %mul.43 = f32[3,768,1024]{2,1,0:T(8,128)} reshape(f32[3,6,128,8,128]{4,3,2,1,0:T(8,128)} %mul.42) | data formatting | bytes 18874368 | tf_op jit(solution)/shard_map/mul | solution.py:41
  23.6 9.1 %multiply_convert_fusion = bf16[3,768,1024]{2,1,0:T(8,128)(2,1)} fusion(f32[3,768,1024]{2,1,0:T(8,128)} %mul.43, bf16[3,768,1024]{2,1,0:T(8,128)(2,1)} %param.10), kind=kLoop, calls=%fused_computation.6 | loop fusion | flops 7077888 | bytes 18874368 | tf_op jit(solution)/shard_map/convert_element_type | solution.py:47
  33.9 15.9 %all-gather.1 = bf16[8,3,3072]{2,1,0:T(4,128)(2,1)S(1)} all-gather(bf16[1,3,3072]{2,1,0:T(4,128)(2,1)S(1)} %select_bitcast_fusion), channel_id=1, replica_groups=mesh['dp'=4,'expert'=8] {'expert'}, dimensions={0}, use_global_device_ids=true | all-gather | bytes 165888 | tf_op jit(solution)/shard_map/all_gather | solution.py:35
  50.6 3.7 %all-to-all-start = ((bf16[24,4,768]{2,0,1:T(8,128)(2,1)}), bf16[24,4,768]{2,0,1:T(8,128)(2,1)S(1)}, u32[]{:S(2)}, u32[]{:S(2)}) async-start(bf16[24,4,768]{2,0,1:T(8,128)(2,1)} %copy.12), calls=%async_computation | async-start | bytes 294912 | tf_op jit(solution)/shard_map/all_to_all | solution.py:70
  55.6 14.1 %all-gather = bf16[8,3,3072]{2,1,0:T(4,128)(2,1)S(1)} all-gather(bf16[1,3,3072]{2,1,0:T(4,128)(2,1)S(1)} %fusion.10), channel_id=1, replica_groups=mesh['dp'=4,'expert'=8] {'expert'}, dimensions={0}, use_global_device_ids=true | all-gather | bytes 165888 | tf_op jit(solution)/shard_map/all_gather | solution.py:36
  72.0 140.3 %all-gather.4.cloned.1.call-done = bf16[3,3072,1024]{2,1,0:T(8,128)(2,1)} async-done(((bf16[3,768,1024]{2,1,0:T(8,128)(2,1)}), bf16[3,3072,1024]{2,1,0:T(8,128)(2,1)}) %all-gather.4.cloned.1.call-update) | async-done | bytes 18874384 | tf_op jit(solution)/shard_map/all_gather | solution.py:46
  212.3 3.9 %fusion = f32[24,1024]{1,0:T(8,128)S(1)} fusion(bf16[24,3072]{1,0:T(8,128)(2,1)S(1)} %reshape.117, bf16[3,3072,1024]{2,1,0:T(8,128)(2,1)} %all-gather.4.cloned.1.call-done), kind=kOutput, calls=%fused_computation.10 | convolution fusion | flops 150994944 | bytes 6537216 | tf_op jit(solution)/shard_map/dot_general | solution.py:51
  216.1 4.3 %fusion.4 = f32[24,1024]{1,0:T(8,128)S(1)} fusion(bf16[24,3072]{1,0:T(8,128)(2,1)S(1)} %reshape.119, bf16[3,3072,1024]{2,1,0:T(8,128)(2,1)} %all-gather.4.cloned.1.call-done), kind=kOutput, calls=%fused_computation.17 | convolution fusion | flops 150994944 | bytes 6537216 | tf_op jit(solution)/shard_map/dot_general | solution.py:49
  220.5 4.5 %multiply_convert_fusion.1 = (bf16[24,1024]{1,0:T(8,128)(2,1)S(1)}, bf16[24,1024]{1,0:T(8,128)(2,1)S(1)}, bf16[24,1024]{1,0:T(8,128)(2,1)S(1)}) fusion(f32[24,1024]{1,0:T(8,128)S(1)} %fusion.4, f32[24,1024]{1,0:T(8,128)S(1)} %fusion, bf16[24,3072]{1,0:T(8,128)(2,1)S(1)} %reshape.119, bf16[3,3072,1024]{2,1,0:T(8,128)(2,1)} %all-gather.4.cloned.1.call-done), kind=kOutput, calls=%fused_computation.23 | convolution fusion | flops 151363584 | bytes 6782976 | tf_op jit(solution)/shard_map/dot_general | solution.py:50
  225.0 1.7 fusion.1
  226.7 1.8 fusion.5
  228.5 31.7 %all-reduce.2 = bf16[24,3072]{1,0:T(8,128)(2,1)S(1)} all-reduce(f32[24,3072]{1,0:T(8,128)S(1)} %fusion.5), channel_id=2, replica_groups=mesh['dp'=4,'expert'=8] {'expert'}, use_global_device_ids=true, to_apply=%region_5.6.clone | all-reduce | flops 73728 | bytes 442368
  260.8 0.7 select_convert_fusion
  261.5 9.0 %all_gather.21 = bf16[96,1024]{1,0:T(8,128)(2,1)S(1)} all-gather(bf16[24,1024]{1,0:T(8,128)(2,1)S(1)} %get-tuple-element.3), channel_id=1, replica_groups=mesh['dp'=4,'expert'=8] {'dp'}, dimensions={0}, use_global_device_ids=true | all-gather | bytes 245760 | tf_op jit(solution)/shard_map/all_gather | solution.py:74
  270.5 7.9 %all_gather.22 = bf16[96,1024]{1,0:T(8,128)(2,1)S(1)} all-gather(bf16[24,1024]{1,0:T(8,128)(2,1)S(1)} %get-tuple-element.4), channel_id=1, replica_groups=mesh['dp'=4,'expert'=8] {'dp'}, dimensions={0}, use_global_device_ids=true | all-gather | bytes 245760 | tf_op jit(solution)/shard_map/all_gather | solution.py:75
  278.3 3.5 %all-to-all-start.1 = ((bf16[24,4,768]{2,0,1:T(8,128)(2,1)}), bf16[24,4,768]{2,0,1:T(8,128)(2,1)S(1)}, u32[]{:S(2)}, u32[]{:S(2)}) async-start(bf16[24,4,768]{2,0,1:T(8,128)(2,1)} %copy.13), calls=%async_computation.1 | async-start | bytes 294912 | tf_op jit(solution)/shard_map/all_to_all | solution.py:71
  281.9 4.5 %convert_bitcast_fusion.1 = bf16[4,1,768,1024]{3,2,0,1:T(8,128)(2,1)} fusion(bf16[4,24,1024]{2,1,0:T(8,128)(2,1)S(1)} %bitcast.58, bf16[24,4,768]{2,0,1:T(8,128)(2,1)S(1)} %all-to-all-done), kind=kOutput, calls=%fused_computation.12 | convolution fusion | flops 154140672 | bytes 6635520 | tf_op jit(solution)/shard_map/rkd,rkh->rdh/dot_general | solution.py:86
  286.4 4.4 %convert_bitcast_fusion.2 = bf16[4,1,768,1024]{3,2,0,1:T(8,128)(2,1)} fusion(bf16[4,24,1024]{2,1,0:T(8,128)(2,1)S(1)} %bitcast.57, bf16[24,4,768]{2,0,1:T(8,128)(2,1)S(1)} %all-to-all-done), kind=kOutput, calls=%fused_computation.13 | convolution fusion | flops 154140672 | bytes 6635520 | tf_op jit(solution)/shard_map/rkd,rkh->rdh/dot_general | solution.py:85
  290.9 9.0 %all_gather.23 = bf16[96,1024]{1,0:T(8,128)(2,1)S(1)} all-gather(bf16[24,1024]{1,0:T(8,128)(2,1)S(1)} %get-tuple-element.2), channel_id=1, replica_groups=mesh['dp'=4,'expert'=8] {'dp'}, dimensions={0}, use_global_device_ids=true | all-gather | bytes 245760 | tf_op jit(solution)/shard_map/all_gather | solution.py:76
  299.9 1.8 convert_bitcast_fusion
  301.7 0.9 copy-done.2
  302.7 11.1 %pad_maximum_fusion = bf16[4,3,768,1024]{3,2,0,1:T(8,128)(2,1)} fusion(bf16[4,1,768,1024]{3,2,0,1:T(8,128)(2,1)S(1)} %convert_bitcast_fusion, bf16[4,1,768,1024]{3,2,0,1:T(8,128)(2,1)S(1)} %copy-done.2, bf16[4,1,768,1024]{3,2,0,1:T(8,128)(2,1)} %convert_bitcast_fusion.2), kind=kLoop, calls=%fused_computation.5 | loop fusion | flops 18874368 | bytes 37748736 | tf_op jit(solution)/shard_map/stack | solution.py:83
  313.7 14.8 %convert_reduce_fusion = f32[3,768,1024]{2,1,0:T(8,128)} fusion(bf16[4,3,768,1024]{3,2,0,1:T(8,128)(2,1)} %pad_maximum_fusion), kind=kLoop, calls=%fused_computation.4 | loop fusion | flops 16515072 | bytes 28311552 | tf_op jit(solution)/shard_map/reduce_sum | solution.py:92
  (44 shorter events, 6.3 us)
Async XLA Ops:
  7.2 25.9 %copy-start = (bf16[12,3072]{1,0:T(8,128)(2,1)S(1)}, bf16[12,3072]{1,0:T(8,128)(2,1)}, u32[]{:S(2)}) copy-start(bf16[12,3072]{1,0:T(8,128)(2,1)} %param.7) | copy-start | bytes 221188
  7.2 205.1 %all-gather.4.cloned.1.call-start = ((), (), s32[]{:S(2)}) async-start(), calls=%async_computation.2 | async-start | bytes 23592960 | tf_op jit(solution)/shard_map/all_gather | solution.py:46
  23.6 9.1 %copy-start.5 = (s32[12,2]{0,1:T(2,128)S(1)}, s32[12,2]{0,1:T(2,128)}, u32[]{:S(2)}) copy-start(s32[12,2]{0,1:T(2,128)} %param.8) | copy-start | bytes 292
  23.6 30.7 %copy-start.6 = (f32[12,2]{0,1:T(2,128)S(1)}, f32[12,2]{0,1:T(2,128)}, u32[]{:S(2)}) copy-start(f32[12,2]{0,1:T(2,128)} %param.9) | copy-start | bytes 292
  23.6 31.4 %copy-start.4 = (bf16[12,3072]{1,0:T(8,128)(2,1)S(1)}, bf16[12,3072]{1,0:T(8,128)(2,1)}, u32[]{:S(2)}) copy-start(bf16[12,3072]{1,0:T(8,128)(2,1)} %param.6) | copy-start | bytes 221188
  23.6 47.2 %copy-start.7 = (u32[32]{0:T(128)S(1)}, u32[32]{0:T(128)}, u32[]{:S(2)}) copy-start(u32[32]{0:T(128)} %constant.34) | copy-start | bytes 388
  50.6 227.8 %all-to-all-start = ((bf16[24,4,768]{2,0,1:T(8,128)(2,1)}), bf16[24,4,768]{2,0,1:T(8,128)(2,1)S(1)}, u32[]{:S(2)}, u32[]{:S(2)}) async-start(bf16[24,4,768]{2,0,1:T(8,128)(2,1)} %copy.12), calls=%async_computation | async-start | bytes 294912 | tf_op jit(solution)/shard_map/all_to_all | solution.py:70
  212.3 12.7 %copy-start.3 = (bf16[3,3072,1024]{2,1,0:T(8,128)(2,1)S(1)}, bf16[3,3072,1024]{2,1,0:T(8,128)(2,1)}, u32[]{:S(2)}) copy-start(bf16[3,3072,1024]{2,1,0:T(8,128)(2,1)} %all-gather.4.cloned.1.call-done) | copy-start | bytes 56623108
  278.3 21.5 %all-to-all-start.1 = ((bf16[24,4,768]{2,0,1:T(8,128)(2,1)}), bf16[24,4,768]{2,0,1:T(8,128)(2,1)S(1)}, u32[]{:S(2)}, u32[]{:S(2)}) async-start(bf16[24,4,768]{2,0,1:T(8,128)(2,1)} %copy.13), calls=%async_computation.1 | async-start | bytes 294912 | tf_op jit(solution)/shard_map/all_to_all | solution.py:71
  299.9 2.8 copy-start.2
  302.7 25.9 %copy-start.1 = (bf16[12,3072]{1,0:T(8,128)(2,1)S(1)}, bf16[12,3072]{1,0:T(8,128)(2,1)}, u32[]{:S(2)}) copy-start(bf16[12,3072]{1,0:T(8,128)(2,1)} %param.7) | copy-start | bytes 221188
Sparse Core Ops, SparseCore 0:
  32.8 179.3 all-gather.3
where the time goes:
time: 336 us; the launch traced here: 335 us
  waiting for transfers between devices  140 us (42%)
  blocking collectives  87.5 us (26%)
  other arithmetic  37.1 us (11%)
  matrix products  27 us (8%)
  local copies, waits for them, and re-layouts  21.4 us (6%)
  between operations  14.8 us (4%)
  starting transfers between devices  7.28 us (2%)
    all_gather x1, waiting for transfers between devices, per_device(): lax.all_gather(scaled.reshape(local_shape).astype(jnp.bfloat16), 'dp', ax...  140 us
    unnamed x1, blocking collectives  31.7 us
    all_gather x1, blocking collectives, per_device(): lax.all_gather(sent_input, 'expert', axis=0, tiled=True)  15.9 us
    mul x2, local copies, waits for them, and re-layouts, per_device(): w_stack.astype(jnp.float32)  15.6 us
    reduce_sum x1, other arithmetic, per_device(): weight_grads = jnp.sum(rounded.astype(jnp.float32), axis=0)  14.8 us
    all_gather x1, blocking collectives, per_device(): lax.all_gather(sent_grad, 'expert', axis=0, tiled=True)  14.1 us
    another operation x1, other arithmetic, per_device(): jnp.stack([jnp.einsum('rkd,rkh->rdh', column_input, gate_all, preferred_e...  11.1 us
    convert_element_type x1, other arithmetic, per_device(): scaled.reshape(local_shape).astype(jnp.bfloat16)  9.1 us
  transfers between devices with their start and end apart: 3, of which 1 were waited for; matrix products, arithmetic and copies ran while one was open for 9% of the time, Pallas kernels for 0%

commit v1 on v0

v1 whole, which is shorter than its diff:
```python
import functools

import jax
import jax.numpy as jnp
from jax import lax
from jax.experimental import pallas as pl
from jax.experimental.pallas import tpu as pltpu
from jax.sharding import PartitionSpec as P

TILE = 128
CAP = 3
BF = jnp.bfloat16
F32 = jnp.float32
VMEM_LIMIT = 60 * 1024 * 1024


def iota(shape, dim):
    return lax.broadcasted_iota(jnp.int32, shape, dim)


def mm(a, b, ca=1, cb=0):
    return lax.dot_general(a, b, (((ca,), (cb,)), ((), ())), preferred_element_type=F32)


def exchange_kernel(
    n_dp, n_ex, chunk,
    og_ref, li_ref, ids_ref, prob_ref, exps_ref, w_hbm,
    xt_ref, act_ref, ig_ref,
    w, slab_out, slabs, x, part_out, part_in, acts, acc, back_out, back_in, own_out, own_in,
    w_sem, s1_send, s1_recv, s2_send, s2_recv, s3_send, s3_recv, rs_send, rs_recv,
    ag_send, ag_recv, b1_send, b1_recv, b2_send, b2_recv,
):
    p, e = lax.axis_index("dp"), lax.axis_index("expert")
    tok, width = og_ref.shape
    _, depth, hid = w.shape
    rows = n_ex * CAP
    n_chunk = hid // chunk
    pairs = n_ex // 2
    z, core = e // 2, e % 2
    partner = 2 * z + 1 - core

    def send(src, dst, ssem, rsem, q, f):
        copy = pltpu.make_async_remote_copy(
            src_ref=src, dst_ref=dst, send_sem=ssem, recv_sem=rsem,
            device_id=(q, f), device_id_type=pl.DeviceIdType.MESH,
        )
        copy.start()
        return copy

    w_copies = [
        pltpu.make_async_copy(w_hbm.at[m], w.at[m], w_sem.at[m]) for m in range(3)
    ]
    for copy in w_copies:
        copy.start()

    barrier = pltpu.get_barrier_semaphore()
    for k in range(1, n_dp):
        pl.semaphore_signal(
            barrier, inc=1, device_id=(lax.rem(p + k, n_dp), e),
            device_id_type=pl.DeviceIdType.MESH,
        )
    for k in range(1, n_ex):
        pl.semaphore_signal(
            barrier, inc=1, device_id=(p, lax.rem(e + k, n_ex)),
            device_id_type=pl.DeviceIdType.MESH,
        )

    routed = ids_ref[...] == 0
    mask = jnp.max(routed.astype(F32), axis=1, keepdims=True)
    prob = jnp.sum(jnp.where(routed, prob_ref[...], 0.0), axis=1, keepdims=True)
    earlier = (iota((tok, tok), 1) <= iota((tok, tok), 0)).astype(F32)
    mask_wide = jnp.broadcast_to(mask, (tok, 128))
    place = mm(earlier, mask_wide) - 1.0
    lane = iota((tok, 128), 1).astype(F32)
    hit_in = jnp.where((place == lane) & (mask_wide > 0.5), 1.0, 0.0)
    hit_gr = jnp.where((place + CAP == lane) & (mask_wide > 0.5), 1.0, 0.0)
    scaled = (og_ref[...].astype(F32) * prob).astype(BF)
    slots = (
        mm(hit_in[:, :8].astype(BF), li_ref[...], 0, 0)
        + mm(hit_gr[:, :8].astype(BF), scaled, 0, 0)
    ).astype(BF)
    for q in range(n_dp):
        slab_out[q] = slots[:, q * depth:(q + 1) * depth]
    pl.semaphore_wait(barrier, n_dp - 1 + n_ex - 1)

    pend = []
    for k in range(1, n_dp):
        q = lax.rem(p + k, n_dp)
        pend.append(send(slab_out.at[q], slabs.at[e, p], s1_send.at[k], s1_recv.at[k], q, e))
    slabs[e, p] = slab_out[p]
    for copy in pend:
        copy.wait()

    pend = [send(slabs.at[e], slabs.at[e], s2_send.at[0], s2_recv.at[0], p, partner)]
    for k in range(1, pairs):
        f = 2 * lax.rem(z + k, pairs) + core
        pend.append(send(slabs.at[e], slabs.at[e], s2_send.at[k], s2_recv.at[k], p, f))

    for copy in w_copies:
        copy.wait()
    tr, tc = depth // TILE, hid // TILE

    def scale_rows(i, carry):
        m, r = i // tr, i % tr
        at = pl.ds(pl.multiple_of(r * TILE, TILE), TILE)
        for j in range(tc):
            power = lax.shift_left(jnp.int32(1), exps_ref[m, r, j] + 15)
            factor = power.astype(F32) * (2.0 ** -15)
            cols = slice(j * TILE, (j + 1) * TILE)
            w[m, at, cols] = (w[m, at, cols].astype(F32) * factor).astype(BF)
        return carry

    lax.fori_loop(0, 3 * tr, scale_rows, 0)

    relays = []
    for k in range(1, pairs):
        pend[k].wait_recv()
        f = 2 * lax.rem(z - k + pairs, pairs) + core
        relays.append(send(slabs.at[f], slabs.at[f], s3_send.at[k], s3_recv.at[k], p, partner))
    pend[0].wait_recv()
    for copy in relays:
        copy.wait_recv()

    src, dst = iota((2 * rows, n_ex * 8), 1), iota((2 * rows, n_ex * 8), 0)
    kind, rest = dst // rows, dst % rows
    pick = jnp.where(
        src == (rest // CAP) * 8 + kind * CAP + rest % CAP, 1.0, 0.0
    ).astype(BF)
    got = [mm(pick, slabs[:, g].reshape(n_ex * 8, depth)) for g in range(n_dp)]
    xs = [
        jnp.concatenate([v[i * rows:(i + 1) * rows] for v in got], axis=0) for i in range(2)
    ]
    for i in range(2):
        x[i] = xs[i].astype(BF)

    sent = []
    for c in range(n_chunk):
        cols = slice(c * chunk, (c + 1) * chunk)
        for m in range(3):
            val = mm(x[m // 2], w[m, :, cols]).astype(F32)
            for g in range(n_dp):
                part_out[c, g, m] = val[g * rows:(g + 1) * rows].astype(BF)
        line = []
        for k in range(1, n_dp):
            q = lax.rem(p + k, n_dp)
            line.append(send(
                part_out.at[c, q], part_in.at[c, k], rs_send.at[c, k], rs_recv.at[c, k], q, e
            ))
        sent.append(line)

    for i in range(2):
        xt_ref[i] = x[i].astype(F32).T.astype(BF)

    shared = []
    for c in range(n_chunk):
        total = [part_out[c, p, m].astype(F32) for m in range(3)]
        for k in range(1, n_dp):
            sent[c][k - 1].wait_recv()
            total = [total[m] + part_in[c, k, m].astype(F32) for m in range(3)]
        gate, up, down = total
        sig = jax.nn.sigmoid(gate)
        act = gate * sig
        acts[c, p, 0] = (down * up * sig * (1.0 + gate * (1.0 - sig))).astype(BF)
        acts[c, p, 1] = (down * act).astype(BF)
        acts[c, p, 2] = (act * up).astype(BF)
        line = []
        for k in range(1, n_dp):
            q = lax.rem(p + k, n_dp)
            line.append(send(
                acts.at[c, p], acts.at[c, p], ag_send.at[c, k], ag_recv.at[c, k], q, e
            ))
        shared.append(line)

    for c in range(n_chunk):
        cols = slice(c * chunk, (c + 1) * chunk)
        for copy in shared[c]:
            copy.wait_recv()
        full = []
        for m in range(3):
            val = jnp.concatenate(
                [acts[c, g, m].astype(F32) for g in range(n_dp)], axis=0
            ).astype(BF)
            act_ref[m, :, cols] = val
            full.append(val)
        part = mm(full[0], w[0, :, cols], 1, 1) + mm(full[1], w[1, :, cols], 1, 1)
        if c == 0:
            acc[...] = part
        else:
            acc[...] += part

    pad = n_dp * 4
    summed = acc[...].astype(BF)
    batch = min(n_ex, 8)
    for b in range(n_ex // batch):
        shape = (batch * pad, n_dp * rows)
        to, frm = iota(shape, 0), iota(shape, 1)
        f, g, c = to // pad + b * batch, (to % pad) // 4, to % 4
        choose = jnp.where(
            (c < CAP) & (frm == g * rows + f * CAP + c), 1.0, 0.0
        ).astype(BF)
        val = mm(choose, summed).astype(BF)
        for j in range(batch):
            back_out[b * batch + j] = val[j * pad:(j + 1) * pad]
    back = []
    for k in range(1, n_ex):
        f = lax.rem(e + k, n_ex)
        back.append(send(back_out.at[f], back_in.at[k], b1_send.at[k], b1_recv.at[k], p, f))
    total = back_out[e].astype(F32)
    for k in range(1, n_ex):
        back[k - 1].wait_recv()
        total = total + back_in[k].astype(F32)
    for g in range(n_dp):
        own_out[g] = total[g * 4:(g + 1) * 4].astype(BF)
    last = []
    for k in range(1, n_dp):
        q = lax.rem(p + k, n_dp)
        last.append(send(own_out.at[q], own_in.at[p], b2_send.at[k], b2_recv.at[k], q, e))
    own_in[p] = own_out[p]
    for copy in last:
        copy.wait_recv()
    for q in range(n_dp):
        ig_ref[:, q * depth:(q + 1) * depth] = mm(
            hit_in[:, :4].astype(BF), own_in[q]
        ).astype(BF)

    for copy in pend[: pairs] + relays + back + last:
        copy.wait_send()
    for line in sent + shared:
        for copy in line:
            copy.wait_send()


def grads_kernel(xt_ref, act_ref, out_ref):
    out_ref[0] = mm(xt_ref[0], act_ref[0])


def per_device(n_dp, n_ex, out_grad, layer_input, expert_ids, gate_prob, w_stack, scale_exps):
    tok, width = out_grad.shape
    _, depth, hid = w_stack.shape
    rows = n_ex * CAP
    total = n_dp * rows
    chunk = min(256, hid)
    n_chunk = hid // chunk
    pad = n_dp * 4
    vm = pl.BlockSpec(memory_space=pltpu.VMEM)
    dma = pltpu.SemaphoreType.DMA
    pairs = n_ex // 2
    xt, act, input_grad = pl.pallas_call(
        functools.partial(exchange_kernel, n_dp, n_ex, chunk),
        out_shape=(
            jax.ShapeDtypeStruct((2, depth, total), BF),
            jax.ShapeDtypeStruct((3, total, hid), BF),
            jax.ShapeDtypeStruct((tok, width), BF),
        ),
        in_specs=[
            vm, vm, vm, vm,
            pl.BlockSpec(memory_space=pltpu.SMEM),
            pl.BlockSpec(memory_space=pl.ANY),
        ],
        out_specs=(vm, vm, vm),
        scratch_shapes=[
            pltpu.VMEM((3, depth, hid), BF),
            pltpu.VMEM((n_dp, 8, depth), BF),
            pltpu.VMEM((n_ex, n_dp, 8, depth), BF),
            pltpu.VMEM((2, total, depth), BF),
            pltpu.VMEM((n_chunk, n_dp, 3, rows, chunk), BF),
            pltpu.VMEM((n_chunk, n_dp, 3, rows, chunk), BF),
            pltpu.VMEM((n_chunk, n_dp, 3, rows, chunk), BF),
            pltpu.VMEM((total, depth), F32),
            pltpu.VMEM((n_ex, pad, depth), BF),
            pltpu.VMEM((n_ex, pad, depth), BF),
            pltpu.VMEM((n_dp, 4, depth), BF),
            pltpu.VMEM((n_dp, 4, depth), BF),
            dma((3,)),
            dma((n_dp,)), dma((n_dp,)),
            dma((pairs,)), dma((pairs,)),
            dma((pairs,)), dma((pairs,)),
            dma((n_chunk, n_dp)), dma((n_chunk, n_dp)),
            dma((n_chunk, n_dp)), dma((n_chunk, n_dp)),
            dma((n_ex,)), dma((n_ex,)),
            dma((n_dp,)), dma((n_dp,)),
        ],
        compiler_params=pltpu.CompilerParams(
            collective_id=0, has_side_effects=True, vmem_limit_bytes=VMEM_LIMIT
        ),
    )(out_grad, layer_input, expert_ids, gate_prob, scale_exps, w_stack)
    wide = min(512, hid)
    weight_grads = pl.pallas_call(
        grads_kernel,
        grid=(3, hid // wide),
        in_specs=[
            pl.BlockSpec((1, depth, total), lambda m, c: (m // 2, 0, 0)),
            pl.BlockSpec((1, total, wide), lambda m, c: (m, 0, c)),
        ],
        out_specs=pl.BlockSpec((1, depth, wide), lambda m, c: (m, 0, c)),
        out_shape=jax.ShapeDtypeStruct((3, depth, hid), F32),
        compiler_params=pltpu.CompilerParams(vmem_limit_bytes=VMEM_LIMIT),
    )(xt, act)
    return input_grad, weight_grads


def solution(mesh):
    in_specs = (
        P(("dp", "expert"), None),
        P(("dp", "expert"), None),
        P(("dp", "expert"), None),
        P(("dp", "expert"), None),
        P(None, "dp", "expert"),
        P(None, "dp", "expert"),
    )
    out_specs = (P(("dp", "expert"), None), P(None, "dp", "expert"))
    return jax.shard_map(
        functools.partial(per_device, mesh.shape["dp"], mesh.shape["expert"]),
        mesh=mesh, in_specs=in_specs, out_specs=out_specs, check_vma=False,
    )
```

time: 336 us -> 52.4 us (0.16)
  waiting for transfers between devices: 140 us -> 0 us
  blocking collectives: 87.5 us -> 0 us
  Pallas kernels: 0 us -> 48.1 us
  other arithmetic: 37.1 us -> 0 us
  matrix products: 27 us -> 0 us
  local copies, waits for them, and re-layouts: 21.4 us -> 3.36 us
  between operations: 14.8 us -> 0.65 us
  starting transfers between devices: 7.28 us -> 0 us
    all_gather x1 -> x0, waiting for transfers between devices: 140 us -> none  [per_device(): lax.all_gather(scaled.reshape(local_shape).astype(jnp.bfloat16), 'dp', ax...]
    all_gather x5 -> x0, blocking collectives: 55.8 us -> none  [the longest x1 15.9 us: per_device(): lax.all_gather(sent_input, 'expert', axis=0, tiled=True)]
    pallas_call x0 -> x2, Pallas kernels: none -> 48.1 us  [the longest x1 41.5 us: per_device(): pl.pallas_call(functools.partial(exchange_kernel, n_dp, n_ex, chunk), out...]
    unnamed x1 -> x0, blocking collectives: 31.7 us -> none
    dot_general x8 -> x0, matrix products: 27 us -> none  [the longest x1 4.55 us: per_device(): jnp.einsum('rkd,rkh->rdh', column_input, up_all, preferred_element_type=j...]
    mul x2 -> x0, local copies, waits for them, and re-layouts: 15.6 us -> none  [per_device(): w_stack.astype(jnp.float32)]
    reduce_sum x3 -> x0, other arithmetic: 14.9 us -> none  [the longest x1 14.8 us: per_device(): weight_grads = jnp.sum(rounded.astype(jnp.float32), axis=0)]
    another operation x2 -> x0, other arithmetic: 11.3 us -> none  [the longest x1 11.1 us: per_device(): jnp.stack([jnp.einsum('rkd,rkh->rdh', column_input, gate_all, preferred_e...]
  transfers between devices with their start and end apart: 3 -> 0, of which waited for: 1 -> 0; matrix products, arithmetic and copies ran while one was open for 9% -> 0% of each run, Pallas kernels for 0% -> 0%
where the time goes in v1:
time: 52.4 us; the launch traced here: 52.1 us
  Pallas kernels  48.1 us (92%)
  local copies, waits for them, and re-layouts  3.36 us (6%)
  between operations  0.65 us (1%)
    pallas_call x1, Pallas kernels, per_device(): pl.pallas_call(functools.partial(exchange_kernel, n_dp, n_ex, chunk), out...  41.5 us
    pallas_call x1, Pallas kernels, per_device(): pl.pallas_call(grads_kernel, grid=(3, hid // wide), in_specs=[pl.BlockSpe...  6.54 us
    unnamed x5, local copies, waits for them, and re-layouts  3.36 us

profile of v1, /device:TPU:0, one launch (start us, length us, event | category | flops | bytes accessed | tf_op | source)
XLA Modules:
  0.0 52.1 jit_solution(8436179661324524734)
XLA Ops:
  0.6 1.4 %copy.8.ids_ref = s32[12,2]{1,0:T(8,128)} copy(s32[12,2]{0,1:T(2,128)} %param.8) | data formatting | bytes 192 | tf_op args[2]
  2.0 1.4 %copy.9.prob_ref = f32[12,2]{1,0:T(8,128)} copy(f32[12,2]{0,1:T(2,128)} %param.9) | data formatting | bytes 192 | tf_op args[3]
  3.3 41.5 %shard_map.77 = (bf16[2,768,96]{2,1,0:T(8,128)(2,1)}, bf16[3,96,1024]{2,1,0:T(8,128)(2,1)}, bf16[12,3072]{1,0:T(8,128)(2,1)}) custom-call(bf16[12,3072]{1,0:T(8,128)(2,1)} %og_ref.1, bf16[12,3072]{1,0:T(8,128)(2,1)} %li_ref.1, s32[12,2]{1,0:T(8,128)} %copy.8.ids_ref, f32[12,2]{1,0:T(8,128)} %copy.9.prob_ref, s32[3,6,8]{2,1,0:T(8,128)} %exps_ref.1, ...), custom_call_target="tpu_custom_call" | custom-call | tf_op jit(solution)/shard_map/pallas_call | solution.py:248
  44.9 0.0 copy-start
  44.9 6.5 %shard_map.78 = f32[3,768,1024]{2,1,0:T(8,128)} custom-call(bf16[2,768,96]{2,1,0:T(8,128)(2,1)} %get-tuple-element.6.xt_ref, bf16[3,96,1024]{2,1,0:T(8,128)(2,1)} %get-tuple-element.7.act_ref), custom_call_target="tpu_custom_call" | custom-call | tf_op jit(solution)/shard_map/pallas_call | solution.py:288
  51.4 0.0 copy-done
  51.4 0.6 %copy.11 = bf16[12,3072]{1,0:T(8,128)(2,1)} copy(bf16[12,3072]{1,0:T(8,128)(2,1)S(1)} %copy-done) | data formatting | bytes 147456
Async XLA Ops:
  44.9 6.5 %copy-start = (bf16[12,3072]{1,0:T(8,128)(2,1)S(1)}, bf16[12,3072]{1,0:T(8,128)(2,1)}, u32[]{:S(2)}) copy-start(bf16[12,3072]{1,0:T(8,128)(2,1)} %get-tuple-element.10) | copy-start | bytes 221188

commit v2 on v1

--- a/solution.py
+++ b/solution.py
@@ -9,6 +9,8 @@
 
 TILE = 128
 CAP = 3
+DIRECT = 64
+TALL = 256
 BF = jnp.bfloat16
 F32 = jnp.float32
 VMEM_LIMIT = 60 * 1024 * 1024
@@ -26,9 +28,9 @@
     n_dp, n_ex, chunk,
     og_ref, li_ref, ids_ref, prob_ref, exps_ref, w_hbm,
     xt_ref, act_ref, ig_ref,
-    w, slab_out, slabs, x, part_out, part_in, acts, acc, back_out, back_in, own_out, own_in,
+    w, slab_out, slabs, x, part_out, part_in, acts, hids, acc, back_out, back_in, own_out, own_in,
     w_sem, s1_send, s1_recv, s2_send, s2_recv, s3_send, s3_recv, rs_send, rs_recv,
-    ag_send, ag_recv, b1_send, b1_recv, b2_send, b2_recv,
+    ag_send, ag_recv, hg_send, hg_recv, b1_send, b1_recv, b2_send, b2_recv,
 ):
     p, e = lax.axis_index("dp"), lax.axis_index("expert")
     tok, width = og_ref.shape
@@ -66,18 +68,17 @@
         )
 
     routed = ids_ref[...] == 0
-    mask = jnp.max(routed.astype(F32), axis=1, keepdims=True)
-    prob = jnp.sum(jnp.where(routed, prob_ref[...], 0.0), axis=1, keepdims=True)
-    earlier = (iota((tok, tok), 1) <= iota((tok, tok), 0)).astype(F32)
-    mask_wide = jnp.broadcast_to(mask, (tok, 128))
-    place = mm(earlier, mask_wide) - 1.0
-    lane = iota((tok, 128), 1).astype(F32)
-    hit_in = jnp.where((place == lane) & (mask_wide > 0.5), 1.0, 0.0)
-    hit_gr = jnp.where((place + CAP == lane) & (mask_wide > 0.5), 1.0, 0.0)
-    scaled = (og_ref[...].astype(F32) * prob).astype(BF)
+    mask = jnp.max(routed.astype(F32), axis=0, keepdims=True)
+    prob = jnp.sum(jnp.where(routed, prob_ref[...], 0.0), axis=0, keepdims=True)
+    earlier = (iota((tok, tok), 0) <= iota((tok, tok), 1)).astype(BF)
+    place = mm(jnp.broadcast_to(mask, (8, tok)).astype(BF), earlier) - 1.0
+    mask_tall = jnp.broadcast_to(mask, (8, tok)) > 0.5
+    row = iota((8, tok), 0).astype(F32)
+    hit_in = jnp.where((place == row) & (row < CAP) & mask_tall, 1.0, 0.0)
+    hit_gr = jnp.where((place + CAP == row) & (row >= CAP) & mask_tall, 1.0, 0.0)
+    row_prob = jnp.sum(hit_gr * prob, axis=1, keepdims=True)
     slots = (
-        mm(hit_in[:, :8].astype(BF), li_ref[...], 0, 0)
-        + mm(hit_gr[:, :8].astype(BF), scaled, 0, 0)
+        mm(hit_in.astype(BF), li_ref[...]) + row_prob * mm(hit_gr.astype(BF), og_ref[...])
     ).astype(BF)
     for q in range(n_dp):
         slab_out[q] = slots[:, q * depth:(q + 1) * depth]
@@ -162,7 +163,7 @@
         act = gate * sig
         acts[c, p, 0] = (down * up * sig * (1.0 + gate * (1.0 - sig))).astype(BF)
         acts[c, p, 1] = (down * act).astype(BF)
-        acts[c, p, 2] = (act * up).astype(BF)
+        hids[c, p] = (act * up).astype(BF)
         line = []
         for k in range(1, n_dp):
             q = lax.rem(p + k, n_dp)
@@ -171,12 +172,20 @@
             ))
         shared.append(line)
 
+    late = []
+    for c in range(n_chunk):
+        for k in range(1, n_dp):
+            q = lax.rem(p + k, n_dp)
+            late.append(send(
+                hids.at[c, p], hids.at[c, p], hg_send.at[c, k], hg_recv.at[c, k], q, e
+            ))
+
     for c in range(n_chunk):
         cols = slice(c * chunk, (c + 1) * chunk)
         for copy in shared[c]:
             copy.wait_recv()
         full = []
-        for m in range(3):
+        for m in range(2):
             val = jnp.concatenate(
                 [acts[c, g, m].astype(F32) for g in range(n_dp)], axis=0
             ).astype(BF)
@@ -198,40 +207,84 @@
         choose = jnp.where(
             (c < CAP) & (frm == g * rows + f * CAP + c), 1.0, 0.0
         ).astype(BF)
-        val = mm(choose, summed).astype(BF)
+        val = mm(choose, summed)
         for j in range(batch):
-            back_out[b * batch + j] = val[j * pad:(j + 1) * pad]
-    back = []
-    for k in range(1, n_ex):
-        f = lax.rem(e + k, n_ex)
-        back.append(send(back_out.at[f], back_in.at[k], b1_send.at[k], b1_recv.at[k], p, f))
-    total = back_out[e].astype(F32)
-    for k in range(1, n_ex):
-        back[k - 1].wait_recv()
-        total = total + back_in[k].astype(F32)
-    for g in range(n_dp):
-        own_out[g] = total[g * 4:(g + 1) * 4].astype(BF)
-    last = []
-    for k in range(1, n_dp):
-        q = lax.rem(p + k, n_dp)
-        last.append(send(own_out.at[q], own_in.at[p], b2_send.at[k], b2_recv.at[k], q, e))
-    own_in[p] = own_out[p]
-    for copy in last:
-        copy.wait_recv()
+            for g in range(n_dp):
+                at = j * pad + g * 4
+                back_out[b * batch + j, g] = val[at:at + 4].astype(BF)
+    back, last = [], []
+    if n_dp * n_ex <= DIRECT:
+        for kf in range(n_ex - 1, -1, -1):
+            for kq in range(n_dp - 1, -1, -1):
+                if kq or kf:
+                    q, f = lax.rem(p + kq, n_dp), lax.rem(e + kf, n_ex)
+                    back.append(send(
+                        back_out.at[f, q], back_in.at[e, p],
+                        b1_send.at[kf, kq], b1_recv.at[kf, kq], q, f,
+                    ))
+        back_in[e, p] = back_out[e, p]
+        for copy in late:
+            copy.wait_recv()
+        for c in range(n_chunk):
+            act_ref[2, :, c * chunk:(c + 1) * chunk] = jnp.concatenate(
+                [hids[c, g].astype(F32) for g in range(n_dp)], axis=0
+            ).astype(BF)
+        for copy in back:
+            copy.wait_recv()
+        for q in range(n_dp):
+            total = back_in[0, q].astype(F32)
+            for f in range(1, n_ex):
+                total = total + back_in[f, q].astype(F32)
+            own_in[q] = total.astype(BF)
+    else:
+        for k in range(1, n_ex):
+            f = lax.rem(e + k, n_ex)
+            back.append(send(back_out.at[f], back_in.at[k], b1_send.at[k, 0], b1_recv.at[k, 0], p, f))
+        total = [back_out[e, g].astype(F32) for g in range(n_dp)]
+        for k in range(1, n_ex):
+            back[k - 1].wait_recv()
+            total = [total[g] + back_in[k, g].astype(F32) for g in range(n_dp)]
+        for g in range(n_dp):
+            own_out[g] = total[g].astype(BF)
+        for k in range(1, n_dp):
+            q = lax.rem(p + k, n_dp)
+            last.append(send(own_out.at[q], own_in.at[p], b2_send.at[k], b2_recv.at[k], q, e))
+        own_in[p] = own_out[p]
+        for copy in last:
+            copy.wait_recv()
+        for copy in late:
+            copy.wait_recv()
+        for c in range(n_chunk):
+            act_ref[2, :, c * chunk:(c + 1) * chunk] = jnp.concatenate(
+                [hids[c, g].astype(F32) for g in range(n_dp)], axis=0
+            ).astype(BF)
     for q in range(n_dp):
         ig_ref[:, q * depth:(q + 1) * depth] = mm(
-            hit_in[:, :4].astype(BF), own_in[q]
+            hit_in[:4].astype(BF), own_in[q], 0, 0
         ).astype(BF)
 
-    for copy in pend[: pairs] + relays + back + last:
+    for copy in pend[:pairs] + relays + late + back + last:
         copy.wait_send()
     for line in sent + shared:
         for copy in line:
             copy.wait_send()
 
 
-def grads_kernel(xt_ref, act_ref, out_ref):
-    out_ref[0] = mm(xt_ref[0], act_ref[0])
+def grads_kernel(tall, xt_ref, act_ref, out_hbm, out, sems):
+    _, depth, hid = out.shape
+    steps = depth // tall
+    copies = []
+    for m in range(3):
+        for r in range(steps):
+            at = slice(r * tall, (r + 1) * tall)
+            out[m, at, :] = mm(xt_ref[m // 2, at, :], act_ref[m])
+            copy = pltpu.make_async_copy(
+                out.at[m, at], out_hbm.at[m, at], sems.at[m * steps + r]
+            )
+            copy.start()
+            copies.append(copy)
+    for copy in copies:
+        copy.wait()
 
 
 def per_device(n_dp, n_ex, out_grad, layer_input, expert_ids, gate_prob, w_stack, scale_exps):
@@ -241,7 +294,7 @@
     total = n_dp * rows
     chunk = min(256, hid)
     n_chunk = hid // chunk
-    pad = n_dp * 4
+    n_last = n_dp if n_dp * n_ex <= DIRECT else 1
     vm = pl.BlockSpec(memory_space=pltpu.VMEM)
     dma = pltpu.SemaphoreType.DMA
     pairs = n_ex // 2
@@ -265,10 +318,11 @@
             pltpu.VMEM((2, total, depth), BF),
             pltpu.VMEM((n_chunk, n_dp, 3, rows, chunk), BF),
             pltpu.VMEM((n_chunk, n_dp, 3, rows, chunk), BF),
-            pltpu.VMEM((n_chunk, n_dp, 3, rows, chunk), BF),
+            pltpu.VMEM((n_chunk, n_dp, 2, rows, chunk), BF),
+            pltpu.VMEM((n_chunk, n_dp, rows, chunk), BF),
             pltpu.VMEM((total, depth), F32),
-            pltpu.VMEM((n_ex, pad, depth), BF),
-            pltpu.VMEM((n_ex, pad, depth), BF),
+            pltpu.VMEM((n_ex, n_dp, 4, depth), BF),
+            pltpu.VMEM((n_ex, n_dp, 4, depth), BF),
             pltpu.VMEM((n_dp, 4, depth), BF),
             pltpu.VMEM((n_dp, 4, depth), BF),
             dma((3,)),
@@ -277,23 +331,24 @@
             dma((pairs,)), dma((pairs,)),
             dma((n_chunk, n_dp)), dma((n_chunk, n_dp)),
             dma((n_chunk, n_dp)), dma((n_chunk, n_dp)),
-            dma((n_ex,)), dma((n_ex,)),
+            dma((n_chunk, n_dp)), dma((n_chunk, n_dp)),
+            dma((n_ex, n_last)), dma((n_ex, n_last)),
             dma((n_dp,)), dma((n_dp,)),
         ],
         compiler_params=pltpu.CompilerParams(
             collective_id=0, has_side_effects=True, vmem_limit_bytes=VMEM_LIMIT
         ),
-    )(out_grad, layer_input, expert_ids, gate_prob, scale_exps, w_stack)
-    wide = min(512, hid)
+    )(out_grad, layer_input, expert_ids.T, gate_prob.T, scale_exps, w_stack)
+    tall = min(TALL, depth)
     weight_grads = pl.pallas_call(
-        grads_kernel,
-        grid=(3, hid // wide),
-        in_specs=[
-            pl.BlockSpec((1, depth, total), lambda m, c: (m // 2, 0, 0)),
-            pl.BlockSpec((1, total, wide), lambda m, c: (m, 0, c)),
+        functools.partial(grads_kernel, tall),
+        in_specs=[vm, vm],
+        out_specs=pl.BlockSpec(memory_space=pl.ANY),
+        out_shape=jax.ShapeDtypeStruct((3, depth, hid), F32),
+        scratch_shapes=[
+            pltpu.VMEM((3, depth, hid), F32),
+            dma((3 * (depth // tall),)),
         ],
-        out_specs=pl.BlockSpec((1, depth, wide), lambda m, c: (m, 0, c)),
-        out_shape=jax.ShapeDtypeStruct((3, depth, hid), F32),
         compiler_params=pltpu.CompilerParams(vmem_limit_bytes=VMEM_LIMIT),
     )(xt, act)
     return input_grad, weight_grads

time: 52.4 us -> 47.3 us (0.903)
  local copies, waits for them, and re-layouts: 3.36 us -> 0.65 us
  Pallas kernels: 48.1 us -> 45.7 us
    unnamed x5 -> x3, local copies, waits for them, and re-layouts: 3.36 us -> 0.65 us
    pallas_call x1, Pallas kernels: 6.54 us -> 5.18 us  [per_device(): pl.pallas_call(functools.partial(grads_kernel, tall), in_specs=[vm, vm],...]
    pallas_call x1, Pallas kernels: 41.5 us -> 40.6 us  [per_device(): pl.pallas_call(functools.partial(exchange_kernel, n_dp, n_ex, chunk), out...]
where the time goes in v2:
time: 47.3 us; the launch traced here: 47.1 us
  Pallas kernels  45.7 us (97%)
  between operations  0.66 us (1%)
  local copies, waits for them, and re-layouts  0.65 us (1%)
    pallas_call x1, Pallas kernels, per_device(): pl.pallas_call(functools.partial(exchange_kernel, n_dp, n_ex, chunk), out...  40.6 us
    pallas_call x1, Pallas kernels, per_device(): pl.pallas_call(functools.partial(grads_kernel, tall), in_specs=[vm, vm],...  5.18 us

profile of v2, /device:TPU:0, one launch (start us, length us, event | category | flops | bytes accessed | tf_op | source)
XLA Modules:
  0.0 47.1 jit_solution(9986645227328515198)
XLA Ops:
  0.6 40.6 %shard_map.77 = (bf16[2,768,96]{2,1,0:T(8,128)(2,1)}, bf16[3,96,1024]{2,1,0:T(8,128)(2,1)}, bf16[12,3072]{1,0:T(8,128)(2,1)}) custom-call(bf16[12,3072]{1,0:T(8,128)(2,1)} %og_ref.1, bf16[12,3072]{1,0:T(8,128)(2,1)} %li_ref.1, s32[2,12]{1,0:T(2,128)} %bitcast.2, f32[2,12]{1,0:T(2,128)} %bitcast.3, s32[3,6,8]{2,1,0:T(8,128)} %exps_ref.1, ...), custom_call_target="tpu_custom_call" | custom-call | tf_op jit(solution)/shard_map/pallas_call | solution.py:301
  41.2 0.0 copy-start
  41.2 5.2 %shard_map.78 = f32[3,768,1024]{2,1,0:T(8,128)} custom-call(bf16[2,768,96]{2,1,0:T(8,128)(2,1)} %get-tuple-element.6.xt_ref, bf16[3,96,1024]{2,1,0:T(8,128)(2,1)} %get-tuple-element.7.act_ref), custom_call_target="tpu_custom_call" | custom-call | tf_op jit(solution)/shard_map/pallas_call | solution.py:343
  46.4 0.0 copy-done
  46.4 0.6 %copy.9 = bf16[12,3072]{1,0:T(8,128)(2,1)} copy(bf16[12,3072]{1,0:T(8,128)(2,1)S(1)} %copy-done) | data formatting | bytes 147456
Async XLA Ops:
  41.2 5.2 %copy-start = (bf16[12,3072]{1,0:T(8,128)(2,1)S(1)}, bf16[12,3072]{1,0:T(8,128)(2,1)}, u32[]{:S(2)}) copy-start(bf16[12,3072]{1,0:T(8,128)(2,1)} %get-tuple-element.10) | copy-start | bytes 221188

commit v3 on v2

--- a/solution.py
+++ b/solution.py
@@ -197,21 +197,29 @@
         else:
             acc[...] += part
 
-    pad = n_dp * 4
+    pad = n_dp * 2
+    half = depth // 2
     summed = acc[...].astype(BF)
     batch = min(n_ex, 8)
     for b in range(n_ex // batch):
         shape = (batch * pad, n_dp * rows)
         to, frm = iota(shape, 0), iota(shape, 1)
-        f, g, c = to // pad + b * batch, (to % pad) // 4, to % 4
-        choose = jnp.where(
-            (c < CAP) & (frm == g * rows + f * CAP + c), 1.0, 0.0
-        ).astype(BF)
-        val = mm(choose, summed)
+        f, g = to // pad + b * batch, (to % pad) // 2
+        parts = []
+        for t in range(CAP):
+            piece = CAP * (to % 2) + t
+            val = 0.0
+            for h in range(2):
+                choose = jnp.where(
+                    (piece % 2 == h) & (frm == g * rows + f * CAP + piece // 2), 1.0, 0.0
+                ).astype(BF)
+                val = val + mm(choose, summed[:, h * half:(h + 1) * half])
+            parts.append(val)
+        val = jnp.concatenate(parts, axis=1)
         for j in range(batch):
             for g in range(n_dp):
-                at = j * pad + g * 4
-                back_out[b * batch + j, g] = val[at:at + 4].astype(BF)
+                at = j * pad + g * 2
+                back_out[b * batch + j, g] = val[at:at + 2].astype(BF)
     back, last = [], []
     if n_dp * n_ex <= DIRECT:
         for kf in range(n_ex - 1, -1, -1):
@@ -259,8 +267,16 @@
                 [hids[c, g].astype(F32) for g in range(n_dp)], axis=0
             ).astype(BF)
     for q in range(n_dp):
+        packed = own_in[q].astype(F32)
+        halves = [
+            packed[j // CAP:j // CAP + 1, (j % CAP) * half:(j % CAP + 1) * half]
+            for j in range(2 * CAP)
+        ]
+        back_rows = jnp.concatenate(
+            [jnp.concatenate(halves[2 * c:2 * c + 2], axis=1) for c in range(CAP)], axis=0
+        ).astype(BF)
         ig_ref[:, q * depth:(q + 1) * depth] = mm(
-            hit_in[:4].astype(BF), own_in[q], 0, 0
+            hit_in[:CAP].astype(BF), back_rows, 0, 0
         ).astype(BF)
 
     for copy in pend[:pairs] + relays + late + back + last:
@@ -321,10 +337,10 @@
             pltpu.VMEM((n_chunk, n_dp, 2, rows, chunk), BF),
             pltpu.VMEM((n_chunk, n_dp, rows, chunk), BF),
             pltpu.VMEM((total, depth), F32),
-            pltpu.VMEM((n_ex, n_dp, 4, depth), BF),
-            pltpu.VMEM((n_ex, n_dp, 4, depth), BF),
-            pltpu.VMEM((n_dp, 4, depth), BF),
-            pltpu.VMEM((n_dp, 4, depth), BF),
+            pltpu.VMEM((n_ex, n_dp, 2, CAP * depth // 2), BF),
+            pltpu.VMEM((n_ex, n_dp, 2, CAP * depth // 2), BF),
+            pltpu.VMEM((n_dp, 2, CAP * depth // 2), BF),
+            pltpu.VMEM((n_dp, 2, CAP * depth // 2), BF),
             dma((3,)),
             dma((n_dp,)), dma((n_dp,)),
             dma((pairs,)), dma((pairs,)),

time: 47.3 us -> 46.7 us (0.987)
  Pallas kernels: 45.7 us -> 45.1 us
    pallas_call x1, Pallas kernels: 40.6 us -> 40 us  [per_device(): pl.pallas_call(functools.partial(exchange_kernel, n_dp, n_ex, chunk), out...]
where the time goes in v3:
time: 46.7 us; the launch traced here: 46.4 us
  Pallas kernels  45.1 us (97%)
  between operations  0.66 us (1%)
  local copies, waits for them, and re-layouts  0.65 us (1%)
    pallas_call x1, Pallas kernels, per_device(): pl.pallas_call(functools.partial(exchange_kernel, n_dp, n_ex, chunk), out...  40 us
    pallas_call x1, Pallas kernels, per_device(): pl.pallas_call(functools.partial(grads_kernel, tall), in_specs=[vm, vm],...  5.18 us

profile of v3, /device:TPU:0, one launch (start us, length us, event | category | flops | bytes accessed | tf_op | source)
XLA Modules:
  0.0 46.4 jit_solution(1074431684281663448)
XLA Ops:
  0.6 40.0 %shard_map.77 = (bf16[2,768,96]{2,1,0:T(8,128)(2,1)}, bf16[3,96,1024]{2,1,0:T(8,128)(2,1)}, bf16[12,3072]{1,0:T(8,128)(2,1)}) custom-call(bf16[12,3072]{1,0:T(8,128)(2,1)} %og_ref.1, bf16[12,3072]{1,0:T(8,128)(2,1)} %li_ref.1, s32[2,12]{1,0:T(2,128)} %bitcast.2, f32[2,12]{1,0:T(2,128)} %bitcast.3, s32[3,6,8]{2,1,0:T(8,128)} %exps_ref.1, ...), custom_call_target="tpu_custom_call" | custom-call | tf_op jit(solution)/shard_map/pallas_call | solution.py:317
  40.6 0.0 copy-start
  40.6 5.2 %shard_map.78 = f32[3,768,1024]{2,1,0:T(8,128)} custom-call(bf16[2,768,96]{2,1,0:T(8,128)(2,1)} %get-tuple-element.6.xt_ref, bf16[3,96,1024]{2,1,0:T(8,128)(2,1)} %get-tuple-element.7.act_ref), custom_call_target="tpu_custom_call" | custom-call | tf_op jit(solution)/shard_map/pallas_call | solution.py:359
  45.8 0.0 copy-done
  45.8 0.6 %copy.9 = bf16[12,3072]{1,0:T(8,128)(2,1)} copy(bf16[12,3072]{1,0:T(8,128)(2,1)S(1)} %copy-done) | data formatting | bytes 147456
Async XLA Ops:
  40.6 5.2 %copy-start = (bf16[12,3072]{1,0:T(8,128)(2,1)S(1)}, bf16[12,3072]{1,0:T(8,128)(2,1)}, u32[]{:S(2)}) copy-start(bf16[12,3072]{1,0:T(8,128)(2,1)} %get-tuple-element.10) | copy-start | bytes 221188
